TPU v7x, 32 devices: a whole 2x2x4 slice. The times are simulated.
32 devices in a mesh: row: 8 (over y, x, core), col: 4 (over z).
Axes of the slice: x: 2, y: 2, z: 4, core: 2. Of those that a mesh axis runs over, the one named last changes fastest.
Arguments:
- choi: float32 [4, 2048, 1024], P(None, 'row', 'col'), may hold values from -0.5 to 8, as said below
Outputs:
- factored: float32 [4, 2048, 1024], P(None, 'row', 'col')
Inputs may be any that keep to these rules, and one draw needn't show every extreme that they name: `choi`: the leading 1024 x 1024 block of the matrix is symmetric with a positive diagonal, and its leading 2 * 256 square is positive definite.
All inputs are finite; a program needn't handle non-finite values.
Results may differ from a plain program's by a relative error of at most 0.0001.
Values sent between devices are 32-bit elements; how exact they have to be, the bound alone decides.
A program may use at most 64 MiB of HBM per device.

v0:
```python
import jax
import jax.numpy as jnp
from jax import lax
from jax.sharding import PartitionSpec as P

PANELS = 2


def broadcast(value, axis, source):
    kept = jnp.where(lax.axis_index(axis) == source, value, 0).astype(value.dtype)
    return lax.psum(kept, axis)


def factor_tile(diagonal):
    tile_size = diagonal.shape[0]
    identity = jnp.eye(tile_size, dtype=jnp.float32)
    factor = jnp.linalg.cholesky(diagonal)
    inverse = jax.scipy.linalg.solve_triangular(factor, identity, lower=True)
    return (factor, inverse)


def panel_from(blocks, factor, inverse, tile_index, step):
    beneath = jnp.einsum("sij,kj->sik", blocks, inverse, precision=lax.Precision.HIGHEST)
    place = tile_index[:, None, None]
    return jnp.where(place > step, beneath, jnp.where(place == step, factor[None], 0.0))


def body(choi):
    slot_count = choi.shape[0]
    row_count = lax.axis_size("row")
    my_row = lax.axis_index("row")
    my_col = lax.axis_index("col")
    tile_index = jnp.arange(slot_count, dtype=jnp.int32) * row_count + my_row
    current = choi
    for step in range(PANELS):
        row_tile = current[step // row_count]
        tile_row = broadcast(row_tile, "row", step % row_count)

        def build(operands):
            factor, inverse = factor_tile(operands[0])
            return panel_from(operands[1], factor, inverse, tile_index, step)

        def nothing(operands):
            return jnp.zeros_like(operands[1])

        panel_tiles = lax.cond(my_col == step, build, nothing, (tile_row, current))
        panel_tiles = broadcast(panel_tiles, "col", step)
        my_tile = lax.dynamic_index_in_dim(panel_tiles, my_col // row_count, 0, keepdims=False)
        partner = broadcast(my_tile, "row", my_col % row_count)
        updated = current - jnp.einsum(
            "sij,kj->sik", panel_tiles, partner, precision=lax.Precision.HIGHEST
        )
        trailing = (tile_index[:, None, None] > step) & (my_col > step)
        current = jnp.where(my_col == step, panel_tiles, jnp.where(trailing, updated, current))
    cleared = (my_col >= PANELS) & (tile_index[:, None, None] < PANELS)
    return jnp.where(cleared, 0.0, current)


def solution(mesh):
    return jax.shard_map(
        body,
        mesh=mesh,
        in_specs=(P(None, "row", "col"),),
        out_specs=P(None, "row", "col"),
        check_vma=False,
    )
```

profile of v0, /device:TPU:30, one launch (start us, length us, event | category | flops | bytes accessed | tf_op | source)
XLA Modules:
  0.0 471.5 jit_solution(8787741748421579258)
XLA Ops:
  6.5 0.0 all-reduce.8.cloned.1.call-start
  6.5 1.7 select_bitcast_fusion.4
  8.2 0.0 all-reduce.8.cloned.1.call-update
  8.2 0.0 all-reduce.10.cloned.1.call-start
  8.3 55.4 %all-reduce.8.cloned.1.call-done = f32[256,256]{1,0:T(8,128)} async-done(((f32[256,256]{1,0:T(8,128)}), f32[256,256]{1,0:T(8,128)}) %all-reduce.8.cloned.1.call-update) | async-done | bytes 262160 | tf_op jit(solution)/shard_map/psum | solution.py:11
  63.7 0.3 conditional.2
  63.7 0.1 broadcast.159.clone
  64.0 1.1 broadcast_select_fusion.1
  65.1 0.0 copy-start
  65.1 0.0 all-reduce.10.cloned.1.call-update
  65.1 0.0 all-reduce.12.cloned.1.call-start
  65.2 111.9 %all-reduce.10.cloned.1.call-done = f32[4,256,256]{2,1,0:T(8,128)} async-done(((f32[4,256,256]{2,1,0:T(8,128)}), f32[4,256,256]{2,1,0:T(8,128)}) %all-reduce.10.cloned.1.call-update) | async-done | bytes 1048592 | tf_op jit(solution)/shard_map/psum | solution.py:11
  177.1 1.7 select_bitcast_fusion.3
  178.7 0.0 all-reduce.12.cloned.1.call-update
  178.8 0.0 all-reduce.14.cloned.1.call-start
  178.8 54.6 %all-reduce.12.cloned.1.call-done = f32[256,256]{1,0:T(8,128)} async-done(((f32[256,256]{1,0:T(8,128)}), f32[256,256]{1,0:T(8,128)}) %all-reduce.12.cloned.1.call-update) | async-done | bytes 262160 | tf_op jit(solution)/shard_map/psum | solution.py:11
  233.5 0.0 copy-done
  233.5 2.7 fusion.32
  236.1 0.7 fusion.33
  236.9 0.0 all-reduce.14.cloned.1.call-update
  236.9 0.0 all-reduce.16.cloned.1.call-start
  236.9 53.4 %all-reduce.14.cloned.1.call-done = f32[256,256]{1,0:T(8,128)} async-done(((f32[256,256]{1,0:T(8,128)}), f32[256,256]{1,0:T(8,128)}) %all-reduce.14.cloned.1.call-update) | async-done | bytes 262160 | tf_op jit(solution)/shard_map/psum | solution.py:11
  290.3 0.4 conditional.3
  290.3 0.1 broadcast.163.clone
  290.7 1.1 broadcast_select_fusion
  291.8 0.0 all-reduce.16.cloned.1.call-update
  291.8 0.0 all-reduce.18.cloned.1.call-start
  291.9 112.9 %all-reduce.16.cloned.1.call-done = f32[4,256,256]{2,1,0:T(8,128)} async-done(((f32[4,256,256]{2,1,0:T(8,128)}), f32[4,256,256]{2,1,0:T(8,128)}) %all-reduce.16.cloned.1.call-update) | async-done | bytes 1048592 | tf_op jit(solution)/shard_map/psum | solution.py:11
  404.8 1.7 select_bitcast_fusion.2
  406.4 0.0 all-reduce.18.cloned.1.call-update
  406.5 54.5 %all-reduce.18.cloned.1.call-done = f32[256,256]{1,0:T(8,128)} async-done(((f32[256,256]{1,0:T(8,128)}), f32[256,256]{1,0:T(8,128)}) %all-reduce.18.cloned.1.call-update) | async-done | bytes 262160 | tf_op jit(solution)/shard_map/psum | solution.py:11
  461.0 3.6 fusion.31
  (3 shorter events, 0.0 us)
Async XLA Ops:
  6.5 57.2 %all-reduce.8.cloned.1.call-start = ((), (), s32[]{:S(2)}) async-start(), calls=%async_computation | async-start | bytes 524288 | tf_op jit(solution)/shard_map/psum | solution.py:11
  8.2 168.8 %all-reduce.10.cloned.1.call-start = ((), (), s32[]{:S(2)}) async-start(), calls=%async_computation.1 | async-start | bytes 2097152 | tf_op jit(solution)/shard_map/psum | solution.py:11
  65.1 168.4 %copy-start = (f32[4,256,256]{2,1,0:T(8,128)S(1)}, f32[4,256,256]{2,1,0:T(8,128)}, u32[]{:S(2)}) copy-start(f32[4,256,256]{2,1,0:T(8,128)} %param.8) | copy-start | bytes 3145732
  65.1 168.3 %all-reduce.12.cloned.1.call-start = ((), (), s32[]{:S(2)}) async-start(), calls=%async_computation.2 | async-start | bytes 524288 | tf_op jit(solution)/shard_map/psum | solution.py:11
  178.8 111.6 %all-reduce.14.cloned.1.call-start = ((), (), s32[]{:S(2)}) async-start(), calls=%async_computation.3 | async-start | bytes 524288 | tf_op jit(solution)/shard_map/psum | solution.py:11
  236.9 167.9 %all-reduce.16.cloned.1.call-start = ((), (), s32[]{:S(2)}) async-start(), calls=%async_computation.4 | async-start | bytes 2097152 | tf_op jit(solution)/shard_map/psum | solution.py:11
  291.8 169.2 %all-reduce.18.cloned.1.call-start = ((), (), s32[]{:S(2)}) async-start(), calls=%async_computation.5 | async-start | bytes 524288 | tf_op jit(solution)/shard_map/psum | solution.py:11
Sparse Core Ops, SparseCore 0:
  10.4 53.2 all-reduce.7
  66.1 110.9 all-reduce.9
  180.1 53.2 all-reduce.11
  237.0 53.2 all-reduce.13
  292.6 112.1 all-reduce.15
  407.7 53.2 all-reduce.17
where the time goes:
time: 475 us; the launch traced here: 472 us
  waiting for transfers between devices  443 us (93%)
  between operations  13.6 us (3%)
  other arithmetic  7.9 us (2%)
  matrix products  6.32 us (1%)
    psum x6, waiting for transfers between devices, broadcast(): return lax.psum(kept, axis)  443 us
  transfers between devices with their start and end apart: 6, of which 6 were waited for; matrix products, arithmetic and copies ran while one was open for 0% of the time, Pallas kernels for 0%

commit v1 on v0

v1 whole, which is shorter than its diff:
```python
import functools

import jax
import jax.numpy as jnp
from jax import lax
from jax.experimental import pallas as pl
from jax.experimental.pallas import tpu as pltpu
from jax.sharding import PartitionSpec as P

MESH = pl.DeviceIdType.MESH
HIGHEST = lax.Precision.HIGHEST
F32 = jnp.float32

TILES = ((0, 0, 0, 4), (1, 0, 1, 2), (1, 1, 1, 2), (0, None, 2, 2), (1, None, 2, 2))
ARRIVAL = (3, 4, 0, 1, 2)
MAX_CHUNKS = 4


def dot(a, b, ca=1, cb=0, precision=HIGHEST):
    return lax.dot_general(
        a, b, (((ca,), (cb,)), ((), ())), precision=precision, preferred_element_type=F32
    )


def pivot_rows(rows, lane, sub, first):
    n = rows.shape[1]
    wide = [jnp.broadcast_to(rows[j : j + 1, :], (8, n)) for j in range(8)]
    columns = [
        jnp.sum(jnp.where(lane == first + j, rows, 0.0), axis=1, keepdims=True) for j in range(8)
    ]
    columns = [jnp.broadcast_to(c, (8, n)) for c in columns]
    entry = [
        [jnp.broadcast_to(columns[j][i : i + 1, :], (8, n)) if j <= i else None for j in range(8)]
        for i in range(8)
    ]
    final = jnp.zeros((8, n), F32)
    for j in range(8):
        here = lane == first + j
        pivot = entry[j][j]
        inverse = 1.0 / pivot
        base = jnp.where(here, 1.0, wide[j])
        final = jnp.where(sub == j, base * lax.rsqrt(pivot), final)
        for i in range(j + 1, 8):
            scale = entry[i][j] * inverse
            wide[i] = jnp.where(here, 0.0, wide[i]) - scale * base
            for t in range(j + 1, i + 1):
                entry[i][t] = entry[i][t] - scale * entry[t][j]
    return final


def invert_factor(z_ref, middle):
    n = z_ref.shape[0]
    lane = lax.broadcasted_iota(jnp.int32, (8, n), 1)
    sub = lax.broadcasted_iota(jnp.int32, (8, n), 0)
    all_lane = lax.broadcasted_iota(jnp.int32, (n, n), 1)
    all_row = lax.broadcasted_iota(jnp.int32, (n, n), 0)

    def group(g, carry):
        first = pl.multiple_of(8 * g, 8)
        final = pivot_rows(z_ref[pl.ds(first, 8), :], lane, sub, first)
        right = jnp.where((lane < first + 8) & (lane > first + sub), 0.0, final)
        left = jnp.where(lane >= first + 8, final, 0.0)
        change = dot(left, right, 0, 0)
        mine = (all_lane >= first) & (all_lane < first + 8) & (all_row >= first + 8)
        z_ref[...] = jnp.where(mine, 0.0, z_ref[...]) - change
        z_ref[pl.ds(first, 8), :] = right
        return carry

    half = n // 16
    lax.fori_loop(0, half, group, 0)
    middle()
    lax.fori_loop(half, n // 8, group, 0)
    z_ref[...] = jnp.where(all_lane <= all_row, z_ref[...], 0.0)


def kernel(
    rows, cols, a_ref, o_ref, tiles, slab, blocks, work, inverse, w_ref,
    tile_send, tile_recv, slab_send, slab_recv,
):
    slots, size, _ = a_ref.shape
    half = size // 2
    r = lax.axis_index("row")
    c = lax.axis_index("col")
    bits = [k for k in range(rows.bit_length()) if (1 << k) < rows][::-1]

    def across(k):
        return r + (1 << k) * (1 - 2 * ((r // (1 << k)) % 2))

    barrier = pltpu.get_barrier_semaphore()
    for k in bits:
        pl.semaphore_signal(barrier, inc=1, device_id=(across(k), c), device_id_type=MESH)

    @pl.when(c > 0)
    def _():
        pl.semaphore_signal(barrier, inc=1, device_id=(r, c - 1), device_id_type=MESH)

    @pl.when(c < cols - 1)
    def _():
        pl.semaphore_signal(barrier, inc=1, device_id=(r, c + 1), device_id_type=MESH)

    peers = len(bits) + jnp.where(c > 0, 1, 0) + jnp.where(c < cols - 1, 1, 0)
    pl.semaphore_wait(barrier, peers)

    def place(t):
        root, owner_col, first_col, chunks = TILES[t]
        q = r if root == 0 else r + 1 - 2 * (r % 2)
        owner = (r == root) & ((c >= first_col) if owner_col is None else (c == owner_col))
        active = c >= first_col
        along = None
        if owner_col is not None:
            along = (r == root) & (c >= owner_col) & (c < cols - 1)
        down = [active & (q % (1 << (k + 1)) == 0) for k in bits]
        return chunks, owner, active & jnp.logical_not(owner), along, down

    def tile_copy(t, chunk, chunks, source, way, device):
        span = pl.ds(chunk * (size // chunks), size // chunks)
        return pltpu.make_async_remote_copy(
            src_ref=source.at[span],
            dst_ref=tiles.at[t, span],
            send_sem=tile_send.at[t, chunk, way],
            recv_sem=tile_recv.at[t, chunk],
            device_id=device,
            device_id_type=MESH,
        )

    def each_send(t, chunk, source, act):
        chunks, _, _, along, down = place(t)
        if along is not None:

            @pl.when(along)
            def _():
                act(tile_copy(t, chunk, chunks, source, 0, (r, c + 1)))

        for n, k in enumerate(bits):

            @pl.when(down[n])
            def _(n=n, k=k):
                act(tile_copy(t, chunk, chunks, source, n + 1, (across(k), c)))

    def slab_copy(which, s, source):
        return pltpu.make_async_remote_copy(
            src_ref=source.at[s],
            dst_ref=slab.at[which, s],
            send_sem=slab_send.at[which, s],
            recv_sem=slab_recv.at[which, s],
            device_id=(r, c + 1),
            device_id_type=MESH,
        )

    def needed(s):
        return (r >= 2) if s == 0 else (r >= 0)

    for t in range(len(TILES)):
        chunks, owner, _, _, _ = place(t)

        @pl.when(owner)
        def _(t=t, chunks=chunks):
            for chunk in range(chunks):
                each_send(t, chunk, a_ref.at[0], lambda copy: copy.start())

    def own_slab(which):
        for s in range(slots):

            @pl.when(needed(s))
            def _(s=s):
                slab_copy(which, s, a_ref).start()

    @pl.when(c == 0)
    def _():
        own_slab(0)

    if cols > 2:

        @pl.when((c == 1) & (r >= 2))
        def _():
            own_slab(1)

    for t in range(len(TILES)):

        @pl.when(place(t)[1])
        def _(t=t):
            tiles[t] = a_ref[0]

    for t in ARRIVAL:
        chunks, _, receives, _, _ = place(t)

        @pl.when(receives)
        def _(t=t, chunks=chunks):
            for chunk in range(chunks):
                tile_copy(t, chunk, chunks, tiles.at[t], 0, (r, c)).wait_recv()
                each_send(t, chunk, tiles.at[t], lambda copy: copy.start())

    if cols > 2:

        @pl.when((c == 1) & (r < 2))
        def _():
            own_slab(1)

    def pass_on(which, s):
        @pl.when(needed(s))
        def _():
            slab_copy(which, s, slab.at[which]).wait_recv()

            @pl.when(c < cols - 1)
            def _():
                slab_copy(which, s, slab.at[which]).start()

    def arrive(position):
        if position < slots:

            @pl.when(c == 1)
            def _():
                pass_on(0, position)

        @pl.when(c >= 2)
        def _():
            pass_on(1 if position < slots else 0, position % slots)

    pending = list(range(2 * slots))

    def take(count):
        for _ in range(min(count, len(pending))):
            arrive(pending.pop(0))

    def block_of(t, i, j):
        return tiles[t, i * half : (i + 1) * half, j * half : (j + 1) * half]

    def load(i, j):
        t = 0 if i < 2 else (1 if j < 2 else 2)
        blocks[i, j] = block_of(t, i % 2, j % 2)

    for i in range(2):
        for j in range(i + 1):
            load(i, j)

    @pl.when(c >= 1)
    def _():
        for i in range(2, 4):
            for j in range(i + 1):
                load(i, j)

    take(2)
    for k in range(4):
        def step(k=k):
            work[...] = blocks[k, k]
            invert_factor(work, lambda: None)

        if k < 2:
            step()
        else:
            pl.when(c >= 1)(step)
        take(1)

        def finish(k=k):
            m = work[...]
            for j in range(k):
                blocks[k, j] = dot(m, blocks[k, j])
            targets = range(k + 1, 4)
            scaled = {i: dot(blocks[i, k], m, 1, 1) for i in targets}
            for i in targets:
                for j in range(k):
                    blocks[i, j] = blocks[i, j] - dot(scaled[i], blocks[k, j])
                blocks[i, k] = -dot(scaled[i], m)
                for j in range(k + 1, i + 1):
                    blocks[i, j] = blocks[i, j] - dot(scaled[i], scaled[j], 1, 1)
            blocks[k, k] = m

        if k < 2:

            @pl.when(c == 0)
            def _(k=k):
                m = work[...]
                if k == 0:
                    scaled = dot(blocks[1, 0], m, 1, 1)
                    blocks[1, 0] = -dot(scaled, m)
                    blocks[1, 1] = blocks[1, 1] - dot(scaled, scaled, 1, 1)
                else:
                    blocks[1, 0] = dot(m, blocks[1, 0])
                blocks[k, k] = m

        pl.when(c >= 1)(finish)

    def gather(n, i, j, zero):
        for x in range(2):
            for y in range(2):
                span = (slice(x * half, (x + 1) * half), slice(y * half, (y + 1) * half))
                if zero and y > x:
                    inverse[(n,) + span] = jnp.zeros((half, half), F32)
                else:
                    inverse[(n,) + span] = blocks[2 * i + x, 2 * j + y]

    lower = lax.broadcasted_iota(jnp.int32, (size, size), 0) >= lax.broadcasted_iota(
        jnp.int32, (size, size), 1
    )
    gather(0, 0, 0, True)

    @pl.when(c >= 1)
    def _():
        gather(1, 1, 0, False)
        gather(2, 1, 1, True)

    @pl.when(c == 0)
    def _():
        for s in range(slots):
            o_ref[s] = dot(a_ref[s], inverse[0], 1, 1)

        @pl.when(r == 0)
        def _():
            o_ref[0] = jnp.where(lower, o_ref[0], 0.0)

    @pl.when(c == 1)
    def _():
        for s in range(slots):
            o_ref[s] = dot(a_ref[s], inverse[2], 1, 1)

        @pl.when(r == 1)
        def _():
            o_ref[0] = jnp.where(lower, o_ref[0] + dot(tiles[1], inverse[1], 1, 1), 0.0)

        @pl.when(r == 0)
        def _():
            o_ref[0] = jnp.zeros((size, size), F32)

    @pl.when(c >= 2)
    def _():
        top = dot(inverse[0], tiles[3])
        low = dot(inverse[1], tiles[3]) + dot(inverse[2], tiles[4])
        w_ref[0] = dot(inverse[0], top, 0, 0) + dot(inverse[1], low, 0, 0)
        w_ref[1] = dot(inverse[2], low, 0, 0)

        @pl.when(r < 2)
        def _():
            o_ref[0] = jnp.zeros((size, size), F32)

    done = 2 * slots - len(pending)
    for position in range(2 * slots):
        if position >= done:
            take(1)
        s = position % slots
        if position < slots:

            @pl.when((c == 1) & needed(s))
            def _(s=s):
                o_ref[s] = o_ref[s] + dot(slab[0, s], inverse[1], 1, 1)

            @pl.when((c >= 2) & needed(s))
            def _(s=s):
                o_ref[s] = a_ref[s] - dot(slab[1, s], w_ref[1])

        else:

            @pl.when((c >= 2) & needed(s))
            def _(s=s):
                o_ref[s] = o_ref[s] - dot(slab[0, s], w_ref[0])

    for t in range(len(TILES)):
        for chunk in range(TILES[t][3]):
            each_send(t, chunk, tiles.at[t], lambda copy: copy.wait_send())
    for s in range(slots):

        @pl.when(needed(s) & (c < cols - 1))
        def _(s=s):
            slab_copy(0, s, a_ref).wait_send()

        @pl.when(needed(s) & (c >= 1) & (c < cols - 1))
        def _(s=s):
            slab_copy(1, s, a_ref).wait_send()


def solution(mesh):
    rows, cols = mesh.shape["row"], mesh.shape["col"]
    ways = rows.bit_length() + 1

    def body(choi):
        slots, size, _ = choi.shape
        half = size // 2
        vmem = pl.BlockSpec(memory_space=pltpu.VMEM)
        return pl.pallas_call(
            functools.partial(kernel, rows, cols),
            out_shape=jax.ShapeDtypeStruct(choi.shape, F32),
            in_specs=[vmem],
            out_specs=vmem,
            scratch_shapes=[
                pltpu.VMEM((len(TILES), size, size), F32),
                pltpu.VMEM((2, slots, size, size), F32),
                pltpu.VMEM((4, 4, half, half), F32),
                pltpu.VMEM((half, half), F32),
                pltpu.VMEM((3, size, size), F32),
                pltpu.VMEM((2, size, size), F32),
                pltpu.SemaphoreType.DMA((len(TILES), MAX_CHUNKS, ways)),
                pltpu.SemaphoreType.DMA((len(TILES), MAX_CHUNKS)),
                pltpu.SemaphoreType.DMA((2, slots)),
                pltpu.SemaphoreType.DMA((2, slots)),
            ],
            compiler_params=pltpu.CompilerParams(collective_id=0, has_side_effects=True),
        )(choi)

    return jax.shard_map(
        body,
        mesh=mesh,
        in_specs=(P(None, "row", "col"),),
        out_specs=P(None, "row", "col"),
        check_vma=False,
    )
```

time: 475 us -> 80.7 us (0.17)
  waiting for transfers between devices: 443 us -> 0 us
  Pallas kernels: 0 us -> 78.2 us
  between operations: 13.6 us -> 0.01 us
  other arithmetic: 7.9 us -> 0 us
  matrix products: 6.32 us -> 0 us
    psum x6 -> x0, waiting for transfers between devices: 443 us -> none  [broadcast(): return lax.psum(kept, axis)]
    pallas_call x0 -> x1, Pallas kernels: none -> 78.2 us  [body(): pl.pallas_call(functools.partial(kernel, rows, cols), out_shape=jax.Shape...]
    select_n x6 -> x0, other arithmetic: 7.87 us -> none  [broadcast(): jnp.where(lax.axis_index(axis) == source, value, 0).astype(value.dtype)]
    dot_general x2 -> x0, matrix products: 6.32 us -> none  [body(): jnp.einsum('sij,kj->sik', panel_tiles, partner, precision=lax.Precision.H...]
  transfers between devices with their start and end apart: 6 -> 0, of which waited for: 6 -> 0; matrix products, arithmetic and copies ran while one was open for 0% -> 0% of each run, Pallas kernels for 0% -> 0%
where the time goes in v1:
time: 80.7 us; the launch traced here: 80.5 us
  Pallas kernels  78.2 us (97%)
  local copies, waits for them, and re-layouts  2.29 us (3%)
    pallas_call x1, Pallas kernels, body(): pl.pallas_call(functools.partial(kernel, rows, cols), out_shape=jax.Shape...  78.2 us
    unnamed x1, local copies, waits for them, and re-layouts  2.29 us

profile of v1, /device:TPU:30, one launch (start us, length us, event | category | flops | bytes accessed | tf_op | source)
XLA Modules:
  0.0 80.5 jit_solution(5411908383136843867)
XLA Ops:
  0.0 78.2 %shard_map.17 = f32[4,256,256]{2,1,0:T(8,128)} custom-call(f32[4,256,256]{2,1,0:T(8,128)} %a_ref.1), custom_call_target="tpu_custom_call" | custom-call | tf_op jit(solution)/shard_map/pallas_call | solution.py:378
  78.2 2.3 %copy.3 = f32[4,256,256]{2,1,0:T(8,128)} copy(f32[4,256,256]{2,1,0:T(8,128)} %shard_map.17) | data formatting | bytes 2097152

commit v2 on v1

--- a/solution.py
+++ b/solution.py
@@ -12,7 +12,6 @@
 F32 = jnp.float32
 
 TILES = ((0, 0, 0, 4), (1, 0, 1, 2), (1, 1, 1, 2), (0, None, 2, 2), (1, None, 2, 2))
-ARRIVAL = (3, 4, 0, 1, 2)
 MAX_CHUNKS = 4
 
 
@@ -20,6 +19,20 @@
     return lax.dot_general(
         a, b, (((ca,), (cb,)), ((), ())), precision=precision, preferred_element_type=F32
     )
+
+
+def split(x):
+    high = x.astype(jnp.bfloat16)
+    return high, (x - high.astype(F32)).astype(jnp.bfloat16)
+
+
+def dot3(a, b):
+    (ah, al), (bh, bl) = a, b
+
+    def one(x, y):
+        return jnp.dot(x, y, preferred_element_type=F32)
+
+    return one(al, bh) + one(ah, bl) + one(ah, bh)
 
 
 def pivot_rows(rows, lane, sub, first):
@@ -48,7 +61,7 @@
     return final
 
 
-def invert_factor(z_ref, middle):
+def invert_factor(z_ref, between):
     n = z_ref.shape[0]
     lane = lax.broadcasted_iota(jnp.int32, (8, n), 1)
     sub = lax.broadcasted_iota(jnp.int32, (8, n), 0)
@@ -66,15 +79,15 @@
         z_ref[pl.ds(first, 8), :] = right
         return carry
 
-    half = n // 16
-    lax.fori_loop(0, half, group, 0)
-    middle()
-    lax.fori_loop(half, n // 8, group, 0)
+    quarter = n // 32
+    for part in range(4):
+        lax.fori_loop(part * quarter, (part + 1) * quarter, group, 0)
+        between(part)
     z_ref[...] = jnp.where(all_lane <= all_row, z_ref[...], 0.0)
 
 
 def kernel(
-    rows, cols, a_ref, o_ref, tiles, slab, blocks, work, inverse, w_ref,
+    rows, cols, a_ref, o_ref, tiles, slab, blocks, work, inverse, rhs, w_high, w_low,
     tile_send, tile_recv, slab_send, slab_recv,
 ):
     slots, size, _ = a_ref.shape
@@ -181,40 +194,44 @@
         def _(t=t):
             tiles[t] = a_ref[0]
 
-    for t in ARRIVAL:
+    def collect(t, which):
         chunks, _, receives, _, _ = place(t)
 
-        @pl.when(receives)
-        def _(t=t, chunks=chunks):
+        @pl.when(receives & which)
+        def _():
             for chunk in range(chunks):
                 tile_copy(t, chunk, chunks, tiles.at[t], 0, (r, c)).wait_recv()
                 each_send(t, chunk, tiles.at[t], lambda copy: copy.start())
 
+    beyond = r + 1 - 2 * (r % 2)
+    depth = sum((beyond // (1 << k)) % 2 for k in bits)
+    for t in (3, 4, 0):
+        collect(t, r >= 0)
+    for t in (1, 2):
+        collect(t, depth == 0)
+
     if cols > 2:
 
         @pl.when((c == 1) & (r < 2))
         def _():
             own_slab(1)
 
+    def land(which, s):
+        slab_copy(which, s, slab.at[which]).wait_recv()
+
     def pass_on(which, s):
-        @pl.when(needed(s))
-        def _():
-            slab_copy(which, s, slab.at[which]).wait_recv()
-
-            @pl.when(c < cols - 1)
-            def _():
-                slab_copy(which, s, slab.at[which]).start()
+        land(which, s)
+        slab_copy(which, s, slab.at[which]).start()
 
     def arrive(position):
+        s = position % slots
+        which = 1 if position < slots else 0
         if position < slots:
-
-            @pl.when(c == 1)
-            def _():
-                pass_on(0, position)
-
-        @pl.when(c >= 2)
-        def _():
-            pass_on(1 if position < slots else 0, position % slots)
+            only = (c == 1) & needed(s)
+            pl.when(only & (c < cols - 1))(lambda: pass_on(0, s))
+            pl.when(only & (c == cols - 1))(lambda: land(0, s))
+        if cols > 3:
+            pl.when((c >= 2) & (c < cols - 1) & needed(s))(lambda: pass_on(which, s))
 
     pending = list(range(2 * slots))
 
@@ -225,31 +242,65 @@
     def block_of(t, i, j):
         return tiles[t, i * half : (i + 1) * half, j * half : (j + 1) * half]
 
-    def load(i, j):
-        t = 0 if i < 2 else (1 if j < 2 else 2)
-        blocks[i, j] = block_of(t, i % 2, j % 2)
-
     for i in range(2):
         for j in range(i + 1):
-            load(i, j)
+            blocks[i, j] = block_of(0, i, j)
 
     @pl.when(c >= 1)
     def _():
         for i in range(2, 4):
-            for j in range(i + 1):
-                load(i, j)
+            for j in range(2, i + 1):
+                blocks[i, j] = jnp.zeros((half, half), F32)
+
+    @pl.when(c >= 2)
+    def _():
+        for i in range(4):
+            rhs[i] = tiles[3 + i // 2, (i % 2) * half : (i % 2 + 1) * half, :]
+
+    during = ((1, 1), (1, 1), (0, 1), (1, 0))
+
+    def between(k, part):
+        if k == 0 and part == 0:
+            collect(1, depth == 1)
+        if k == 0 and part == 2:
+            collect(1, depth == 2)
+        if k == 0 and part == 3:
+            collect(1, depth >= 3)
+            collect(2, depth == 1)
+        if k == 1 and part == 1:
+            collect(2, depth == 2)
+        if k == 1 and part == 3:
+            collect(2, depth >= 3)
+        if part == 1:
+            take(during[k][0])
 
     take(2)
     for k in range(4):
+        if k == 2:
+
+            @pl.when(c >= 1)
+            def _():
+                for i in range(2, 4):
+                    for j in range(2, i + 1):
+                        blocks[i, j] = blocks[i, j] + block_of(2, i - 2, j - 2)
+
         def step(k=k):
             work[...] = blocks[k, k]
-            invert_factor(work, lambda: None)
+            invert_factor(work, lambda part: between(k, part))
 
         if k < 2:
             step()
         else:
             pl.when(c >= 1)(step)
-        take(1)
+        take(during[k][1])
+        if k == 0:
+
+            @pl.when(c >= 1)
+            def _():
+                for i in range(2, 4):
+                    for j in range(2):
+                        blocks[i, j] = block_of(1, i - 2, j)
+
 
         def finish(k=k):
             m = work[...]
@@ -278,7 +329,21 @@
                     blocks[1, 0] = dot(m, blocks[1, 0])
                 blocks[k, k] = m
 
-        pl.when(c >= 1)(finish)
+        pl.when(c == 1)(finish)
+
+        @pl.when(c >= 2)
+        def _(k=k):
+            m = work[...]
+            scaled = {i: dot(blocks[i, k], m, 1, 1) for i in range(k + 1, 4)}
+            for i in scaled:
+                for j in range(k + 1, i + 1):
+                    blocks[i, j] = blocks[i, j] - dot(scaled[i], scaled[j], 1, 1)
+                blocks[i, k] = scaled[i]
+            blocks[k, k] = m
+            y = dot(m, rhs[k])
+            for i in scaled:
+                rhs[i] = rhs[i] - dot(scaled[i], y)
+            rhs[k] = y
 
     def gather(n, i, j, zero):
         for x in range(2):
@@ -292,9 +357,11 @@
     lower = lax.broadcasted_iota(jnp.int32, (size, size), 0) >= lax.broadcasted_iota(
         jnp.int32, (size, size), 1
     )
-    gather(0, 0, 0, True)
-
-    @pl.when(c >= 1)
+    @pl.when(c == 0)
+    def _():
+        gather(0, 0, 0, True)
+
+    @pl.when(c == 1)
     def _():
         gather(1, 1, 0, False)
         gather(2, 1, 1, True)
@@ -323,14 +390,20 @@
 
     @pl.when(c >= 2)
     def _():
-        top = dot(inverse[0], tiles[3])
-        low = dot(inverse[1], tiles[3]) + dot(inverse[2], tiles[4])
-        w_ref[0] = dot(inverse[0], top, 0, 0) + dot(inverse[1], low, 0, 0)
-        w_ref[1] = dot(inverse[2], low, 0, 0)
-
-        @pl.when(r < 2)
-        def _():
-            o_ref[0] = jnp.zeros((size, size), F32)
+        w = {}
+        for k in reversed(range(4)):
+            x = rhs[k]
+            for i in range(k + 1, 4):
+                x = x - dot(blocks[i, k], w[i], 0, 0)
+            w[k] = dot(blocks[k, k], x, 0, 0)
+            high, low = split(w[k])
+            span = slice((k % 2) * half, (k % 2 + 1) * half)
+            w_high[k // 2, span, :] = high
+            w_low[k // 2, span, :] = low
+
+    @pl.when((c >= 2) & (r < 2))
+    def _():
+        o_ref[0] = a_ref[0]
 
     done = 2 * slots - len(pending)
     for position in range(2 * slots):
@@ -343,15 +416,23 @@
             def _(s=s):
                 o_ref[s] = o_ref[s] + dot(slab[0, s], inverse[1], 1, 1)
 
+            @pl.when((c >= 2) & (c == cols - 1) & needed(s))
+            def _(s=s):
+                land(1, s)
+
             @pl.when((c >= 2) & needed(s))
             def _(s=s):
-                o_ref[s] = a_ref[s] - dot(slab[1, s], w_ref[1])
+                o_ref[s] = a_ref[s] - dot3(split(slab[1, s]), (w_high[1], w_low[1]))
 
         else:
 
+            @pl.when((c >= 2) & (c == cols - 1) & needed(s))
+            def _(s=s):
+                land(0, s)
+
             @pl.when((c >= 2) & needed(s))
             def _(s=s):
-                o_ref[s] = o_ref[s] - dot(slab[0, s], w_ref[0])
+                o_ref[s] = o_ref[s] - dot3(split(slab[0, s]), (w_high[0], w_low[0]))
 
     for t in range(len(TILES)):
         for chunk in range(TILES[t][3]):
@@ -375,7 +456,7 @@
         slots, size, _ = choi.shape
         half = size // 2
         vmem = pl.BlockSpec(memory_space=pltpu.VMEM)
-        return pl.pallas_call(
+        result = pl.pallas_call(
             functools.partial(kernel, rows, cols),
             out_shape=jax.ShapeDtypeStruct(choi.shape, F32),
             in_specs=[vmem],
@@ -386,7 +467,9 @@
                 pltpu.VMEM((4, 4, half, half), F32),
                 pltpu.VMEM((half, half), F32),
                 pltpu.VMEM((3, size, size), F32),
-                pltpu.VMEM((2, size, size), F32),
+                pltpu.VMEM((4, half, size), F32),
+                pltpu.VMEM((2, size, size), jnp.bfloat16),
+                pltpu.VMEM((2, size, size), jnp.bfloat16),
                 pltpu.SemaphoreType.DMA((len(TILES), MAX_CHUNKS, ways)),
                 pltpu.SemaphoreType.DMA((len(TILES), MAX_CHUNKS)),
                 pltpu.SemaphoreType.DMA((2, slots)),
@@ -394,6 +477,9 @@
             ],
             compiler_params=pltpu.CompilerParams(collective_id=0, has_side_effects=True),
         )(choi)
+        tile_row = jnp.arange(slots, dtype=jnp.int32) * rows + lax.axis_index("row")
+        cleared = (lax.axis_index("col") >= 2) & (tile_row[:, None, None] < 2)
+        return jnp.where(cleared, 0.0, result)
 
     return jax.shard_map(
         body,

time: 80.7 us -> 70.9 us (0.88)
  Pallas kernels: 78.2 us -> 67.8 us
  other arithmetic: 0 us -> 2.37 us
  local copies, waits for them, and re-layouts: 2.29 us -> 0 us
    pallas_call x1, Pallas kernels: 78.2 us -> 67.8 us  [body(): pl.pallas_call(functools.partial(kernel, rows, cols), out_shape=jax.Shape...]
    select_n x0 -> x1, other arithmetic: none -> 2.36 us  [body(): return jnp.where(cleared, 0.0, result)]
    unnamed x1 -> x0, local copies, waits for them, and re-layouts: 2.29 us -> none
where the time goes in v2:
time: 70.9 us; the launch traced here: 70.2 us
  Pallas kernels  67.8 us (96%)
  other arithmetic  2.37 us (3%)
    pallas_call x1, Pallas kernels, body(): pl.pallas_call(functools.partial(kernel, rows, cols), out_shape=jax.Shape...  67.8 us
    select_n x1, other arithmetic, body(): return jnp.where(cleared, 0.0, result)  2.36 us

profile of v2, /device:TPU:30, one launch (start us, length us, event | category | flops | bytes accessed | tf_op | source)
XLA Modules:
  0.0 70.2 jit_solution(3095143956779853427)
XLA Ops:
  0.0 67.8 %shard_map.17 = f32[4,256,256]{2,1,0:T(8,128)} custom-call(f32[4,256,256]{2,1,0:T(8,128)} %a_ref.1), custom_call_target="tpu_custom_call" | custom-call | tf_op jit(solution)/shard_map/pallas_call | solution.py:459
  67.8 2.4 %broadcast_select_fusion = f32[4,256,256]{2,1,0:T(8,128)} fusion(f32[4,256,256]{2,1,0:T(8,128)} %shard_map.17, pred[4]{0:T(512)(128)(4,1)S(1)} %compare_and_fusion), kind=kLoop, calls=%fused_computation | loop fusion | flops 262144 | bytes 2097156 | tf_op jit(solution)/shard_map/jit(_where)/select_n | solution.py:482
  (1 shorter events, 0.0 us)
